TPU v7x, 128 devices: a whole 4x4x4 slice. The times are simulated.
128 devices in a mesh: dp: 16 (over y, z), tensor: 8 (over x, core).
Axes of the slice: x: 4, y: 4, z: 4, core: 2. Of those that a mesh axis runs over, the one named last changes fastest.
Arguments:
- hidden: bfloat16 [3072, 4096], P('dp'), may hold values from -64 to 64
- output_weight: bfloat16 [4096, 128256], P(None, ('dp', 'tensor')), may hold values from -0.109375 to 0.109375
- targets: int32 [3072], P('dp'), may hold values from 0 to 128255
- labels: int32 [3072, 1], P('dp'), may hold values from 0 to 63; in each aligned block of 192 rows (0 to 191, 192 to 383, ...) at most 12 rows name the same one
- prev_scores: float32 [64], P('dp'), may hold values from -12 to 320
- prev_probs: float32 [64], P('dp')
- next_domains: int32 [256], P('dp'), may hold values from 0 to 63
Outputs:
- token_loss: float32 [3072], P(('dp', 'tensor'))
- new_scores: float32 [64], P('dp')
- log_probs: float32 [64], replicated
- sample_weights: float32 [256], P('dp')
Inputs may be any that keep to these rules, and one draw needn't show every extreme that they name: `labels`: within the 192 tokens of one index of dp no domain appears more than 12 times; every domain appears somewhere in the batch.
All inputs are finite; a program needn't handle non-finite values.
Results may differ from a plain program's by a relative error of at most 0.0003.
Values may be sent and summed in bfloat16 or wider, within the bound.
A program may use at most 128 MiB of HBM per device.

v0:
```python
import math

import jax
import jax.numpy as jnp
from jax import lax
from jax.sharding import Mesh
from jax.sharding import PartitionSpec as P

K = 64
STEP = 2000
DP = ("dp_0", "dp_1")
TENSOR = ("tensor_0", "tensor_1")
DP_TENSOR = ("dp_0", "dp_1", "tensor_0", "tensor_1")


def collected_together(value, axis):
    leaves = jax.tree.leaves(value)
    order = sorted(range(len(leaves)), key=lambda k: -leaves[k].size)
    width = (1, *leaves[order[0]].shape)[-1]
    lines = [
        jnp.pad(leaves[k].reshape(-1), (0, -leaves[k].size % width)).reshape(-1, width)
        for k in order
    ]
    both, at, found = (lax.all_gather(jnp.concatenate(lines), axis), 0, {})
    for k, line in zip(order, lines):
        piece = both[:, at : at + len(line)].reshape(len(both), -1)
        found[k] = piece[:, : leaves[k].size].reshape(-1, *leaves[k].shape)
        at += len(line)
    numbers = iter(range(len(leaves)))
    return jax.tree.map(lambda _: found[next(numbers)], value)


def merged_by_axis(value, axes, combine):
    for axis in axes:
        pieces = collected_together(value, axis)
        value = jax.tree.map(lambda part: part[0], pieces)
        for k in range(1, lax.axis_size(axis)):
            value = combine(value, jax.tree.map(lambda part: part[k], pieces))
    return value


def copy_for_each(value, axis):
    devices = lax.axis_size(axis)
    return lax.all_to_all(
        jnp.broadcast_to(value[None], (devices, *value.shape)), axis, 0, 0, tiled=True
    )


def taken_together(value, axis):
    everything = copy_for_each(value, axis)
    return jnp.sum(everything, axis=0)


def packed_total(arrays, axis):
    ends = [0]
    for a in arrays:
        ends.append(ends[-1] + a.size)
    so_far = taken_together(jnp.concatenate([a.ravel() for a in arrays]), axis)
    return tuple((so_far[b:e].reshape(a.shape) for a, b, e in zip(arrays, ends, ends[1:])))


def in_order(blocks, dim):
    blocks = jnp.moveaxis(blocks, 0, dim)
    dims = blocks.shape
    return blocks.reshape(*dims[:dim], dims[dim] * dims[dim + 1], *dims[dim + 2 :])


def gathered_copies(value, axis, dim):
    blocks = copy_for_each(value, axis)
    return in_order(blocks, dim)


def exploration_rates():
    earlier = min(1.0 / K, math.sqrt(math.log(K) / (K * (STEP - 1))))
    current = min(1.0 / K, math.sqrt(math.log(K) / (K * STEP)))
    return (earlier, current)


def block_stats(logits, wanted, vocab_offset):
    largest = jnp.max(logits, axis=1)
    expsum = jnp.sum(jnp.exp(logits - largest[:, None]), axis=1)
    columns = lax.broadcasted_iota(jnp.int32, logits.shape, 1)
    picked = jnp.sum(jnp.where(columns == (wanted - vocab_offset)[:, None], logits, 0.0), axis=1)
    return (largest, expsum, picked)


def join_stats(first, second):
    largest = jnp.maximum(first[0], second[0])
    expsum = first[1] * jnp.exp(first[0] - largest) + second[1] * jnp.exp(second[0] - largest)
    return (largest, expsum, first[2] + second[2])


def body(hidden, output_weight, targets, labels, prev_scores, prev_probs, next_domains):
    local_tokens = hidden.shape[0]
    vocab_local = output_weight.shape[1]
    dp_count = lax.axis_size(DP)
    tensor_count = lax.axis_size(TENSOR)
    vocab_offset = lax.axis_index(DP_TENSOR) * vocab_local
    row_block = lax.all_gather(hidden, DP, axis=0, tiled=True)
    wanted = lax.all_gather(targets, DP, axis=0, tiled=True)
    logits = jnp.dot(row_block, output_weight, preferred_element_type=jnp.float32)
    fresh = block_stats(logits, wanted, vocab_offset)
    largest, expsum, picked = tuple((value for value in fresh))
    share = local_tokens // tensor_count
    largest, expsum, picked = merged_by_axis((largest, expsum, picked), DP_TENSOR, join_stats)
    every_loss = largest + jnp.log(expsum) - picked
    group_loss = lax.dynamic_slice_in_dim(
        every_loss, lax.axis_index(DP) * local_tokens, local_tokens, 0
    )
    token_loss = lax.dynamic_slice_in_dim(group_loss, lax.axis_index(TENSOR) * share, share, 0)
    domains = labels[:, 0]
    onehot = (domains[:, None] == jnp.arange(K, dtype=jnp.int32)[None, :]).astype(jnp.float32)
    owned = K // dp_count
    totals = jnp.dot(group_loss, onehot, precision=lax.Precision.HIGHEST)
    counts = jnp.sum(onehot, axis=0)
    totals, counts = packed_total((totals, counts), DP)
    own_sum = lax.dynamic_slice_in_dim(totals, lax.axis_index(DP) * owned, owned, 0)
    own_count = lax.dynamic_slice_in_dim(counts, lax.axis_index(DP) * owned, owned, 0)
    earlier, current = exploration_rates()
    new_scores = current / earlier * prev_scores + current * (own_sum / own_count) / prev_probs
    every_score = gathered_copies(new_scores, DP, 0)
    largest_score = jnp.max(every_score)
    weights = jnp.exp(every_score - largest_score)
    probs = (1.0 - K * current) * (weights / jnp.sum(weights)) + current
    log_probs = jnp.log(probs)
    chosen = jnp.sum(
        jnp.where(
            next_domains[:, None] == jnp.arange(K, dtype=jnp.int32)[None, :], probs[None, :], 0.0
        ),
        axis=1,
    )
    sample_weights = 1.0 / (K * chosen)
    return (token_loss, new_scores, log_probs, sample_weights)


def solution(mesh):
    torus = Mesh(mesh.devices.reshape(4, 4, 4, 2), ("dp_0", "dp_1", "tensor_0", "tensor_1"))
    return jax.shard_map(
        body,
        mesh=torus,
        in_specs=(P(DP, None), P(None, DP_TENSOR), P(DP), P(DP, None), P(DP), P(DP), P(DP)),
        out_specs=(P(DP_TENSOR), P(DP), P(), P(DP)),
        check_vma=False,
    )
```

profile of v0, /device:TPU:1, one launch (start us, length us, event | category | flops | bytes accessed | tf_op | source)
XLA Modules:
  0.0 277.6 jit_solution(7699041858974375671)
XLA Ops:
  7.2 0.0 all-gather.10.cloned.1.call-start
  7.2 0.7 all-gather.10.cloned.1.call-update
  7.9 1.2 dynamic-slice
  9.8 0.9 dynamic-update-slice
  10.7 64.5 %all-reduce = s32[3072]{0:T(1024)S(1)} all-reduce(s32[3072]{0:T(1024)S(1)} %dynamic-update-slice), channel_id=1, replica_groups=mesh['dp_0'=4,'dp_1'=4,'tensor_0'=4,'tensor_1'=2] {'dp_0','dp_1'}, use_global_device_ids=true, to_apply=%add | all-reduce | flops 3072 | bytes 24576
  75.2 0.8 convert_reduce_fusion
  76.0 92.3 %all-gather.10.cloned.1.call-done = bf16[3072,4096]{1,0:T(8,128)(2,1)} async-done(((bf16[192,4096]{1,0:T(8,128)(2,1)}), bf16[3072,4096]{1,0:T(8,128)(2,1)}) %all-gather.10.cloned.1.call-update) | async-done | bytes 25165840 | tf_op jit(solution)/shard_map/all_gather | solution.py:99
  168.3 31.6 %fusion.48 = (f32[3072]{0:T(1024)S(1)}, f32[3072,1002]{0,1:T(8,128)S(1)}) fusion(bf16[3072,4096]{1,0:T(8,128)(2,1)} %all-gather.10.cloned.1.call-done, bf16[4096,1002]{0,1:T(8,128)(2,1)} %param.8), kind=kOutput, calls=%fused_computation.100 | convolution fusion | flops 25219231744 | bytes 45699072 | tf_op jit(solution)/shard_map/dot_general | solution.py:101
  200.0 0.0 copy-start.3
  200.0 0.0 copy-start.1
  200.0 0.0 copy-start.2
  200.0 0.0 copy-start.4
  200.0 3.4 %exponential_reduce_fusion = (f32[3072]{0:T(1024)S(1)}, f32[3072]{0:T(1024)S(1)}) fusion(f32[3072,1002]{0,1:T(8,128)S(1)} %get-tuple-element.20, f32[3072]{0:T(1024)S(1)} %get-tuple-element.19, s32[3072]{0:T(1024)S(1)} %broadcast_subtract_fusion), kind=kLoop, calls=%fused_computation.2 | loop fusion | flops 15384576 | bytes 12361728 | tf_op jit(solution)/shard_map/reduce_sum | solution.py:81
  203.4 9.7 %all-gather.4 = f32[4,3,3072]{2,1,0:T(4,128)S(1)} all-gather(f32[1,3,3072]{2,1,0:T(4,128)S(1)} %maximum_bitcast_fusion), channel_id=2, replica_groups=mesh['dp_0'=4,'dp_1'=4,'tensor_0'=4,'tensor_1'=2] {'dp_0'}, dimensions={0}, use_global_device_ids=true | all-gather | bytes 184320 | tf_op jit(solution)/shard_map/all_gather | solution.py:24
  213.1 0.1 fusion.23
  213.3 9.2 %all-gather.5 = f32[4,3,3072]{2,1,0:T(4,128)S(1)} all-gather(f32[1,3,3072]{2,1,0:T(4,128)S(1)} %maximum_bitcast_fusion.1), channel_id=3, replica_groups=mesh['dp_0'=4,'dp_1'=4,'tensor_0'=4,'tensor_1'=2] {'dp_1'}, dimensions={0}, use_global_device_ids=true | all-gather | bytes 184320 | tf_op jit(solution)/shard_map/all_gather | solution.py:24
  222.6 0.1 fusion.13
  222.8 9.5 %all-gather.6 = f32[4,3,3072]{2,1,0:T(4,128)S(1)} all-gather(f32[1,3,3072]{2,1,0:T(4,128)S(1)} %maximum_bitcast_fusion.2), channel_id=4, replica_groups=mesh['dp_0'=4,'dp_1'=4,'tensor_0'=4,'tensor_1'=2] {'tensor_0'}, dimensions={0}, use_global_device_ids=true | all-gather | bytes 184320 | tf_op jit(solution)/shard_map/all_gather | solution.py:24
  232.4 0.1 fusion.3
  232.6 10.7 %all-gather.7 = f32[2,3,3072]{2,1,0:T(4,128)S(1)} all-gather(f32[1,3,3072]{2,1,0:T(4,128)S(1)} %maximum_bitcast_fusion.3), channel_id=5, replica_groups=mesh['dp_0'=4,'dp_1'=4,'tensor_0'=4,'tensor_1'=2] {'tensor_1'}, dimensions={0}, use_global_device_ids=true | all-gather | bytes 110592 | tf_op jit(solution)/shard_map/all_gather | solution.py:24
  243.4 0.1 dynamic_slice.16
  243.5 0.0 copy-done.3
  243.5 0.1 convolution_bitcast_fusion
  243.6 0.1 pad_maximum_fusion
  243.7 0.6 broadcast_in_dim.17
  244.3 4.7 %all-to-all-start = ((f32[16,1,128]{2,1,0:T(1,128)}), f32[16,1,128]{2,1,0:T(1,128)S(1)}, u32[]{:S(2)}, u32[]{:S(2)}) async-start(f32[16,1,128]{2,1,0:T(1,128)} %broadcast_in_dim.17), calls=%async_computation | async-start | bytes 16384 | tf_op jit(solution)/shard_map/all_to_all | solution.py:44
  249.0 6.4 %all-to-all-done = f32[16,1,128]{2,1,0:T(1,128)S(1)} async-done(((f32[16,1,128]{2,1,0:T(1,128)}), f32[16,1,128]{2,1,0:T(1,128)S(1)}, u32[]{:S(2)}, u32[]{:S(2)}) %all-to-all-start) | async-done | bytes 8224 | tf_op jit(solution)/shard_map/all_to_all | solution.py:44
  255.4 0.1 fusion.47
  255.5 0.0 copy-done.1
  255.5 0.0 copy-done.2
  255.5 0.1 divide_add_fusion
  255.6 0.0 copy-start
  255.6 0.6 broadcast_in_dim.18
  256.2 3.5 %all-to-all-start.1 = ((f32[16,1,4]{2,1,0:T(1,128)}), f32[16,1,4]{2,1,0:T(1,128)S(1)}, u32[]{:S(2)}, u32[]{:S(2)}) async-start(f32[16,1,4]{2,1,0:T(1,128)} %broadcast_in_dim.18), calls=%async_computation.1 | async-start | bytes 16384 | tf_op jit(solution)/shard_map/all_to_all | solution.py:44
  259.7 0.6 dynamic_slice.15
  260.3 5.8 %all-to-all-done.1 = f32[16,1,4]{2,1,0:T(1,128)S(1)} async-done(((f32[16,1,4]{2,1,0:T(1,128)}), f32[16,1,4]{2,1,0:T(1,128)S(1)}, u32[]{:S(2)}, u32[]{:S(2)}) %all-to-all-start.1) | async-done | bytes 288 | tf_op jit(solution)/shard_map/all_to_all | solution.py:44
  266.1 0.1 copy.13
  266.2 0.6 reduce_max.19
  266.8 1.3 fusion.42
  268.0 1.3 multiply_add_fusion
  269.3 0.1 copy.14
  269.4 0.1 reshape.788
  269.5 0.5 log.7
  270.0 0.0 copy-done.4
  270.0 0.2 select_reduce_fusion.1
  270.2 0.5 multiply_divide_fusion
  270.8 0.0 copy-done
  (12 shorter events, 0.4 us)
Async XLA Ops:
  7.2 161.2 %all-gather.10.cloned.1.call-start = ((), (), s32[]{:S(2)}) async-start(), calls=%async_computation.2 | async-start | bytes 26738688 | tf_op jit(solution)/shard_map/all_gather | solution.py:99
  200.0 43.5 %copy-start.3 = (s32[192,1]{0,1:T(1,128)S(1)}, s32[192,1]{0,1:T(1,128)}, u32[]{:S(2)}) copy-start(s32[192,1]{0,1:T(1,128)} %param.10) | copy-start | bytes 2308
  200.0 55.5 %copy-start.1 = (f32[4]{0:T(128)S(1)}, f32[4]{0:T(128)}, u32[]{:S(2)}) copy-start(f32[4]{0:T(128)} %param.12) | copy-start | bytes 52
  200.0 55.5 %copy-start.2 = (f32[4]{0:T(128)S(1)}, f32[4]{0:T(128)}, u32[]{:S(2)}) copy-start(f32[4]{0:T(128)} %param.11) | copy-start | bytes 52
  200.0 70.1 %copy-start.4 = (s32[16]{0:T(128)S(1)}, s32[16]{0:T(128)}, u32[]{:S(2)}) copy-start(s32[16]{0:T(128)} %param.13) | copy-start | bytes 196
  244.3 11.1 %all-to-all-start = ((f32[16,1,128]{2,1,0:T(1,128)}), f32[16,1,128]{2,1,0:T(1,128)S(1)}, u32[]{:S(2)}, u32[]{:S(2)}) async-start(f32[16,1,128]{2,1,0:T(1,128)} %broadcast_in_dim.17), calls=%async_computation | async-start | bytes 16384 | tf_op jit(solution)/shard_map/all_to_all | solution.py:44
  255.6 15.2 %copy-start = (f32[4]{0:T(128)}, f32[4]{0:T(128)S(1)}, u32[]{:S(2)}) copy-start(f32[4]{0:T(128)S(1)} %divide_add_fusion) | copy-start | bytes 52
  256.2 9.9 %all-to-all-start.1 = ((f32[16,1,4]{2,1,0:T(1,128)}), f32[16,1,4]{2,1,0:T(1,128)S(1)}, u32[]{:S(2)}, u32[]{:S(2)}) async-start(f32[16,1,4]{2,1,0:T(1,128)} %broadcast_in_dim.18), calls=%async_computation.1 | async-start | bytes 16384 | tf_op jit(solution)/shard_map/all_to_all | solution.py:44
Sparse Core Ops, SparseCore 0:
  10.2 158.1 all-gather.9
where the time goes:
time: 280 us; the launch traced here: 278 us
  waiting for transfers between devices  105 us (38%)
  blocking collectives  104 us (37%)
  matrix products  31.7 us (11%)
  between operations  14.9 us (5%)
  other arithmetic  8.98 us (3%)
  starting transfers between devices  8.21 us (3%)
  local copies, waits for them, and re-layouts  4.93 us (2%)
    all_gather x1, waiting for transfers between devices, body(): row_block = lax.all_gather(hidden, DP, axis=0, tiled=True)  92.3 us
    unnamed x1, blocking collectives  64.5 us
    all_gather x4, blocking collectives, collected_together(): both, at, found = (lax.all_gather(jnp.concatenate(lines), axis), 0, {})  39.2 us
    dot_general x1, matrix products, body(): jnp.dot(row_block, output_weight, preferred_element_type=jnp.float32)  31.6 us
    all_to_all x2, waiting for transfers between devices, copy_for_each(): lax.all_to_all(jnp.broadcast_to(value[None], (devices, *value.shape)), ax...  12.2 us
    all_to_all x2, starting transfers between devices, copy_for_each(): lax.all_to_all(jnp.broadcast_to(value[None], (devices, *value.shape)), ax...  8.17 us
  transfers between devices with their start and end apart: 3, of which 3 were waited for; matrix products, arithmetic and copies ran while one was open for 1% of the time, Pallas kernels for 0%

commit v1 on v0

v1 whole, which is shorter than its diff:
```python
import functools
import math

import jax
import jax.numpy as jnp
from jax import lax
from jax.experimental import pallas as pl
from jax.experimental.pallas import tpu as pltpu
from jax.sharding import Mesh
from jax.sharding import PartitionSpec as P

K = 64
STEP = 2000
N = 4
HALF = 96
COLS = 1002
WIDE = 4096
DP = ("y", "z")
TENSOR = ("x", "c")
ALL = ("y", "z", "x", "c")
DIRS = ("+y", "-y", "+z", "-z")
F32 = jnp.float32
NT = (((1,), (1,)), ((), ()))
CUT = 512


ORDER = [
    (0, 0), (0, 1), (0, 3), (1, 0), (3, 0), (1, 3), (3, 1), (1, 1),
    (3, 3), (0, 2), (2, 0), (1, 2), (2, 1), (2, 3), (3, 2), (2, 2),
]
POS = {s: k for k, s in enumerate(ORDER)}
LAST_SLOT = [2, 5, 7, 10, 13, 15]
GROUPS = len(LAST_SLOT)
ROWS_G = 256
N_W = 8


def group_of(slot):
    return next(g for g, k in enumerate(LAST_SLOT) if slot <= k)


def moved(n, d):
    k = 1 if d[0] == "+" else -1
    return ((n[0] + (k if d[1] == "y" else 0)) % N, (n[1] + (k if d[1] == "z" else 0)) % N)


def neg(n):
    return ((-n[0]) % N, (-n[1]) % N)


def children(rot, n):
    axis, sign = rot // 2, 1 - 2 * (rot % 2)
    a, b = n if axis == 0 else n[::-1]
    a, b = (a * sign) % N, (b * sign) % N
    first, second = ("y", "z") if axis == 0 else ("z", "y")
    fwd, back = ("+", "-") if sign == 1 else ("-", "+")
    out = []
    if b == 0:
        if a in (0, 1):
            out.append(fwd + first)
        if a == 0:
            out.append(back + first)
    if b in (0, 1):
        out.append(fwd + second)
    if b == 0:
        out.append(back + second)
    return out


def x_dir(rot):
    return "+x" if rot < 2 else "-x"


def due(role, rot, n, hop, step):
    own = step * (group_of(POS[neg(n)]) + 1)
    out = own
    for d in children(rot, n):
        out = min(out, due(role, rot, moved(n, d), hop, step) - hop)
    if role == "M" and n != (0, 0):
        out = min(out, own - hop)
    return out


def plan(T=1.45, L=2.1, hop=4.5, step=4.0, half=1.32, horizon=1.6, w_ready=15.0, t0=1.2):
    here = {((0, 0), role, rot): 0.0 for role in "CMO" for rot in range(4)}
    todo = {d: [] for d in DIRS + ("+x", "-x")}
    for role in "CM":
        for rot in range(4):
            for n in ORDER:
                for d in children(rot, n):
                    todo[d].append((due(role, rot, moved(n, d), hop, step), neg(n), role, rot))
                if role == "M" and n != (0, 0):
                    late = step * (group_of(POS[neg(n)]) + 1)
                    todo[x_dir(rot)].append((late, neg(n), role, rot))
    end = {d: 0.0 for d in todo}
    chunks = [(g, w) for g in range(GROUPS) for w in range(2)]
    program, t, w_sent = [], t0, 0

    def service(t):
        nonlocal w_sent
        if w_sent < N_W:
            program.append(("w", w_sent))
            w_sent += 1
        for d in todo:
            while end[d] < t + horizon:
                ready = [
                    (late, here[s, role, rot], s, role, rot)
                    for late, s, role, rot in todo[d]
                    if here.get((s, role, rot), 1e9) <= t
                ]
                if not ready:
                    break
                late, _, s, role, rot = min(ready)
                todo[d].remove((late, s, role, rot))
                end[d] = max(t + 0.05, end[d]) + T
                if d[1] == "x":
                    here[s, "O", rot] = end[d] + L
                else:
                    here[neg(moved(neg(s), d)), role, rot] = end[d] + L
                program.append(("send", d, role, rot, s))

    def ready_at(g, w):
        last = max(
            here.get((s, role, rot), 1e9)
            for s in ORDER[: LAST_SLOT[g] + 1]
            for role in "CMO"
            for rot in range(4)
        )
        return max(last, w_ready if w else 3.5)

    while any(todo.values()) or chunks:
        service(t)
        now = [c for c in chunks if ready_at(*c) <= t]
        if now:
            chunks.remove(now[0])
            program.append(("half", *now[0], 0))
            t += half
            service(t)
            program.append(("half", *now[0], 1))
            t += half
        else:
            later = [v for v in here.values() if t < v < 1e8]
            later += [e - horizon for e in end.values() if e - horizon > t]
            later += [v for v in (ready_at(*c) for c in chunks) if t < v < 1e8]
            t = min(later) + 0.01
    return program


def segments():
    have = {((0, 0), role, rot) for role in "CMO" for rot in range(4)}
    done, flags, told = [], set(), 0
    parts, ops = [], []
    ready_stats = []

    def need(s, role, rot):
        if (s, role, rot) not in have:
            have.add((s, role, rot))
            ops.append(("wait", s, role, rot))

    for op in plan():
        if op[0] == "send":
            need(op[4], op[2], op[3])
            ops.append(op)
        elif op[0] == "w":
            ops.append(op)
        else:
            _, g, w, h = op
            if h == 0:
                if "meta" not in flags:
                    flags.add("meta")
                    ops.append(("meta",))
                if w not in flags:
                    flags.add(w)
                    ops.append(("w_wait", w))
                for s in ORDER[: LAST_SLOT[g] + 1]:
                    for role in "CMO":
                        for rot in range(4):
                            need(s, role, rot)
                done.append((g, w))
            parts.append(ops)
            ops = ready_stats
            ready_stats = []
            if h == 1:
                both = [k for k in range(GROUPS) if (k, 0) in done and (k, 1) in done]
                while told < len(both) and both[told] == told:
                    ops.append(("merge", told))
                    lo = 8 * told
                    for k in range(16):
                        if 3 * k + 2 < lo + 8 and 3 * k + 2 >= lo:
                            ops.append(("stat", k))
                            ready_stats.append(("stat_send", k))
                    told += 1
    parts.append(ops)
    parts[-1] += ready_stats
    return done, parts


def rates():
    earlier = min(1.0 / K, math.sqrt(math.log(K) / (K * (STEP - 1))))
    current = min(1.0 / K, math.sqrt(math.log(K) / (K * STEP)))
    return earlier, current


def sum_lanes(v):
    return jnp.sum(v, axis=1, keepdims=True)


def kernel(
    hid, wt, tgt, lab, psc, ppr, nxt,
    o_loss, o_score, o_log, o_weight,
    hbuf, wbuf, meta_out, meta_in, two, trow, cols, sbuf, merged, st_out, st_in, xs_out, xs_in, lo_out, lo_in,
    h_load, w_load, h_send, h_recv, w_send, w_recv, meta_send, meta_recv, st_send, st_recv, xs_send, xs_recv,
    lo_send, lo_recv,
):
    my, mz, mx, mc = (lax.axis_index(a) for a in ALL)
    par = lax.rem(mx, 2)

    def device(dy=0, dz=0, dx=0, dc=0):
        return {
            "y": lax.rem(my + dy, N),
            "z": lax.rem(mz + dz, N),
            "x": lax.rem(mx + dx, N),
            "c": lax.rem(mc + dc, 2),
        }

    def remote(src, dst, send, recv, to):
        return pltpu.make_async_remote_copy(
            src_ref=src, dst_ref=dst, send_sem=send, recv_sem=recv, device_id=to,
            device_id_type=pl.DeviceIdType.MESH,
        )

    def wait_for(ref, sem):
        pltpu.make_async_copy(ref, ref, sem).wait()

    loads = []
    for rg in range(3):
        for kq in range(4):
            rows = pl.ds(pl.multiple_of(mc * HALF + rg * 32, 32), 32)
            loads.append(
                pltpu.make_async_copy(
                    hid.at[rows, pl.ds(kq * 1024, 1024)], hbuf.at[POS[0, 0] * 3 + rg, kq], h_load.at[rg * 4 + kq]
                )
            )
    for load in loads:
        load.start()
    own_w = pltpu.make_async_copy(wt, wbuf.at[0], w_load)
    own_w.start()

    barrier = pltpu.get_barrier_semaphore()
    plane = [(dy, dz, dc) for dy in range(N) for dz in range(N) for dc in range(2) if (dy, dz, dc) != (0, 0, 0)]
    for dy, dz, dc in plane:
        pl.semaphore_signal(barrier, inc=1, device_id=device(dy, dz, 0, dc), device_id_type=pl.DeviceIdType.MESH)
    for dx in range(1, N):
        pl.semaphore_signal(barrier, inc=1, device_id=device(0, 0, dx), device_id_type=pl.DeviceIdType.MESH)

    lane = lax.broadcasted_iota(jnp.int32, (8, 128), 1)
    two[...] = jnp.zeros_like(two)
    two[0:1, 0:192] = tgt[...]
    two[1:2, 0:192] = lab[...]
    both = two[...]
    first = jnp.where(lane < HALF, both[:, :128], -1).astype(F32)
    second = jnp.where(lane < HALF, pltpu.roll(both, 256 - HALF, 1)[:, :128], -1).astype(F32)
    meta_out[...] = jnp.zeros_like(meta_out)
    meta_out[0:1] = jnp.where(mc == 0, first[0:1], second[0:1])
    meta_out[1:2] = first[1:2]
    meta_out[2:3] = second[1:2]
    meta_out[3:4, 0:4] = psc[...]
    meta_out[4:5, 0:4] = ppr[...]
    meta_in[POS[0, 0]] = meta_out[...]
    for load in loads:
        load.wait()
    pl.semaphore_wait(barrier, len(plane) + N - 1)

    for s in ORDER[1:]:
        k = POS[neg(s)]
        remote(meta_out, meta_in.at[k], meta_send, meta_recv.at[k], device(s[0], s[1])).start()

    def piece(slot, role, rot):
        rg = {"C": 0, "M": 1 + par, "O": 2 - par}[role]
        return hbuf.at[slot * 3 + rg, rot], (slot * 3 + rg, rot)

    half_sub = lax.broadcasted_iota(jnp.int32, (K, 128), 0)
    half_lane = lax.broadcasted_iota(jnp.int32, (K, 128), 1)

    def do_meta():
        for k in range(1, 16):
            wait_for(meta_in.at[k], meta_recv.at[k])
        wide_lane = lax.broadcasted_iota(jnp.int32, (8, 256), 1)
        rows = [jnp.zeros((8, 256), F32) for _ in range(GROUPS)]
        counts = jnp.zeros((K, 128), F32)
        score = jnp.zeros((K, 128), F32)
        prob = jnp.zeros((K, 128), F32)
        for k, s in enumerate(ORDER):
            tile = meta_in[k]
            wide = jnp.concatenate([tile, tile], axis=1)
            at = 3 * k
            g, off = at // 8, 32 * (at % 8)
            n = min(3, 8 - at % 8)
            turned = pltpu.roll(wide, off, 1) if off else wide
            rows[g] = jnp.where((wide_lane >= off) & (wide_lane < off + 32 * n), turned, rows[g])
            if n < 3:
                turned = pltpu.roll(wide, 256 - 32 * n, 1)
                rows[g + 1] = jnp.where(wide_lane < 32 * (3 - n), turned, rows[g + 1])
            sub = half_sub.astype(F32)
            for r in (1, 2):
                counts += jnp.where(tile[r : r + 1] == sub, 1.0, 0.0)
            dp = lax.rem(my + s[0], N) * N + lax.rem(mz + s[1], N)
            mine = (half_lane == half_sub - 4 * dp) & (half_lane < 4)
            score += jnp.where(mine, tile[3:4], 0.0)
            prob += jnp.where(mine, tile[4:5], 0.0)
        for g in range(GROUPS):
            trow[g] = rows[g].astype(jnp.int32)
        for i, v in enumerate((counts, score, prob)):
            cols[i] = jnp.broadcast_to(sum_lanes(v), (K, 128))

    def run(ops):
        for op in ops:
            if op[0] == "wait":
                _, s, role, rot = op
                ref, (i, r) = piece(POS[s], role, rot)
                wait_for(ref, h_recv.at[i, r])
            elif op[0] == "send":
                _, d, role, rot, s = op
                src, _ = piece(POS[s], role, rot)
                step = 1 if d[0] == "+" else N - 1
                if d[1] == "x":
                    dst, (i, r) = piece(POS[s], role, rot)
                    to = device(dx=step)
                else:
                    dst, (i, r) = piece(POS[neg(moved(neg(s), d))], role, rot)
                    to = device(dy=step) if d[1] == "y" else device(dz=step)
                remote(src, dst, h_send, h_recv.at[i, r], to).start()
            elif op[0] == "w":
                rows = pl.ds(op[1] * 128, min(128, COLS - op[1] * 128))
                remote(
                    wt.at[rows], wbuf.at[1, rows], w_send.at[op[1]], w_recv.at[op[1]], device(dc=1)
                ).start()
            elif op[0] == "w_wait":
                if op[1] == 0:
                    own_w.wait()
                else:
                    for i in range(N_W):
                        rows = pl.ds(i * 128, min(128, COLS - i * 128))
                        wait_for(wbuf.at[1, rows], w_recv.at[i])
            elif op[0] == "meta":
                do_meta()
            elif op[0] == "merge":
                a, b = sbuf[op[1], 0], sbuf[op[1], 1]
                top = jnp.maximum(a[0:1], b[0:1])
                merged[op[1], 0:1] = top
                merged[op[1], 1:2] = a[1:2] * jnp.exp(a[0:1] - top) + b[1:2] * jnp.exp(b[0:1] - top)
                merged[op[1], 2:3] = a[2:3] + b[2:3]
            elif op[0] == "stat":
                k = op[1]
                at = 3 * k
                g, off = at // 8, 32 * (at % 8)
                n = min(3, 8 - at % 8)
                tile = merged[g]
                msg = (pltpu.roll(tile, 256 - off, 1) if off else tile)[:, :128]
                if n < 3:
                    msg = jnp.where(lane < 32 * n, msg, pltpu.roll(merged[g + 1], 32 * n, 1)[:, :128])
                if ORDER[k] == (0, 0):
                    st_in[k] = msg
                else:
                    st_out[k] = msg
            elif op[0] == "stat_send":
                k = op[1]
                s = ORDER[k]
                if s != (0, 0):
                    i = POS[neg(s)]
                    remote(st_out.at[k], st_in.at[i], st_send, st_recv.at[i], device(s[0], s[1])).start()

    base = ((my * N + mz) * 8 + mx * 2) * COLS
    chunks, parts = segments()
    run(parts[0])

    def stats(g, w, lo, hi, target):
        rhs = jnp.concatenate([hbuf[pl.ds(8 * g, 8), kq].reshape(ROWS_G, 1024) for kq in range(4)], axis=1)
        logits = lax.dot_general(wbuf[w, lo:hi], rhs, NT, preferred_element_type=F32)
        top = jnp.max(logits, axis=0, keepdims=True)
        total = jnp.sum(jnp.exp(logits - top), axis=0, keepdims=True)
        row = lax.broadcasted_iota(jnp.int32, logits.shape, 0) + lo
        picked = jnp.sum(jnp.where(row == target, logits, 0.0), axis=0, keepdims=True)
        return top, total, picked

    def of(j, values):
        if all(v == k // 2 for k, v in enumerate(values)):
            return j // 2
        if all(v == k % 2 for k, v in enumerate(values)):
            return j % 2
        out = 0
        for k, v in enumerate(values):
            if v:
                out += jnp.where(j == k, v, 0)
        return out

    def chunk(j, _):
        for k in range(1, len(chunks)):
            if parts[2 * k]:
                pl.when(j == k)(functools.partial(run, parts[2 * k]))
        g, w = of(j, [c[0] for c in chunks]), of(j, [c[1] for c in chunks])
        core = jnp.where(w == 0, mc, 1 - mc)
        target = trow[g][0:1] - (base + core * COLS)
        a = stats(g, w, 0, CUT, target)
        for k in range(len(chunks)):
            if parts[2 * k + 1]:
                pl.when(j == k)(functools.partial(run, parts[2 * k + 1]))
        b = stats(g, w, CUT, COLS, target)
        top = jnp.maximum(a[0], b[0])
        sbuf[g, w, 0:1] = top
        sbuf[g, w, 1:2] = a[1] * jnp.exp(a[0] - top) + b[1] * jnp.exp(b[0] - top)
        sbuf[g, w, 2:3] = a[2] + b[2]
        return 0

    lax.fori_loop(0, len(chunks), chunk, 0)
    run(parts[-1])

    for k in range(1, 16):
        wait_for(st_in.at[k], st_recv.at[k])

    def joined(tiles):
        top = functools.reduce(jnp.maximum, [t[0:1] for t in tiles])
        total = functools.reduce(jnp.add, [t[1:2] * jnp.exp(t[0:1] - top) for t in tiles])
        return top, total, functools.reduce(jnp.add, [t[2:3] for t in tiles])

    for i, v in enumerate(joined([st_in[k] for k in range(16)])):
        xs_out[i : i + 1] = v
    for dx in range(1, N):
        remote(xs_out, xs_in.at[N - dx], xs_send, xs_recv.at[N - dx], device(dx=dx)).start()
    xs_in[0] = xs_out[...]
    for dx in range(1, N):
        wait_for(xs_in.at[dx], xs_recv.at[dx])
    top, total, picked = joined([xs_in[dx] for dx in range(N)])
    loss = top + jnp.log(total) - picked
    lo_out[...] = loss
    for dy, dz, dc in plane:
        i = POS[neg((dy, dz))] * 2 + dc
        remote(lo_out, lo_in.at[i], lo_send, lo_recv.at[i], device(dy, dz, 0, dc)).start()
    lo_in[0] = lo_out[...]
    for i in range(1, 32):
        wait_for(lo_in.at[i], lo_recv.at[i])

    sums = jnp.zeros((K, 128), F32)
    sub = half_sub.astype(F32)
    for k in range(16):
        tile = meta_in[k]
        for dc in range(2):
            labels = jnp.where(lax.rem(mc + dc, 2) == 0, tile[1:2], tile[2:3])
            sums += jnp.where(labels == sub, lo_in[2 * k + dc], 0.0)
    sums = jnp.broadcast_to(sum_lanes(sums), (K, 128))
    earlier, current = rates()
    score = current / earlier * cols[1] + current * (sums / cols[0]) / cols[2]
    weight = jnp.exp(score - jnp.max(score, axis=0, keepdims=True))
    probs = (1.0 - K * current) * (weight / jnp.sum(weight, axis=0, keepdims=True)) + current
    log_probs = jnp.log(probs)
    dp = my * N + mz

    def across(mask, v):
        return jnp.sum(jnp.where(mask, v, 0.0), axis=0, keepdims=True)

    o_score[...] = across(half_lane == half_sub - 4 * dp, score)[:, :4]
    o_log[...] = across(half_lane == half_sub, log_probs)[:, :K]
    two[2:3, 0:16] = nxt[...]
    chosen = across(two[2:3, :128] == half_sub, probs)
    o_weight[...] = (1.0 / (K * chosen))[:, :16]
    loss = jnp.where(mx // 2 == mc, lo_in[0], lo_in[1])
    loss = jnp.broadcast_to(loss, (8, 128))
    out = loss
    for q in range(1, 4):
        out = jnp.where(2 * lax.rem(mx, 2) + mc == q, pltpu.roll(loss, 128 - 24 * q, 1), out)
    o_loss[...] = out[0:1, :24]

    wait_for(hbuf.at[pl.ds(0, 45)], h_send)
    for i in range(N_W):
        rows = pl.ds(i * 128, min(128, COLS - i * 128))
        wait_for(wbuf.at[1, rows], w_send.at[i])
    wait_for(meta_in.at[pl.ds(0, 15)], meta_send)
    wait_for(st_in.at[pl.ds(0, 15)], st_send)
    wait_for(xs_in.at[pl.ds(0, 3)], xs_send)
    wait_for(lo_in.at[pl.ds(0, 31)], lo_send)


def body(hidden, output_weight, targets, labels, prev_scores, prev_probs, next_domains):
    dma = pltpu.SemaphoreType.DMA
    vmem = pl.BlockSpec(memory_space=pltpu.VMEM)
    outs = pl.pallas_call(
        kernel,
        out_shape=[jax.ShapeDtypeStruct((1, n), F32) for n in (24, 4, K, 16)],
        in_specs=[pl.BlockSpec(memory_space=pl.ANY)] * 2 + [vmem] * 5,
        out_specs=[vmem] * 4,
        scratch_shapes=[
            pltpu.VMEM((48, 4, 32, 1024), jnp.bfloat16),
            pltpu.VMEM((2, COLS, WIDE), jnp.bfloat16),
            pltpu.VMEM((8, 128), F32),
            pltpu.VMEM((16, 8, 128), F32),
            pltpu.VMEM((8, 256), jnp.int32),
            pltpu.VMEM((GROUPS, 8, 256), jnp.int32),
            pltpu.VMEM((3, K, 128), F32),
            pltpu.VMEM((GROUPS, 2, 8, 256), F32),
            pltpu.VMEM((GROUPS, 8, 256), F32),
            pltpu.VMEM((16, 8, 128), F32),
            pltpu.VMEM((16, 8, 128), F32),
            pltpu.VMEM((8, 128), F32),
            pltpu.VMEM((N, 8, 128), F32),
            pltpu.VMEM((1, 128), F32),
            pltpu.VMEM((32, 1, 128), F32),
            dma((12,)),
            dma(()),
            dma(()),
            dma((48, 4)),
            dma((N_W,)),
            dma((N_W,)),
            dma(()),
            dma((16,)),
            dma(()),
            dma((16,)),
            dma(()),
            dma((N,)),
            dma(()),
            dma((32,)),
        ],
        compiler_params=pltpu.CompilerParams(
            collective_id=0, has_side_effects=True, vmem_limit_bytes=56 * 1024 * 1024
        ),
    )(
        hidden,
        output_weight.T,
        targets.reshape(1, -1),
        labels.reshape(1, -1),
        prev_scores.reshape(1, -1),
        prev_probs.reshape(1, -1),
        next_domains.reshape(1, -1),
    )
    return tuple(o.reshape(-1) for o in outs)


def solution(mesh):
    torus = Mesh(mesh.devices.reshape(N, N, N, 2), ALL)
    return jax.shard_map(
        body,
        mesh=torus,
        in_specs=(P(DP, None), P(None, ALL), P(DP), P(DP, None), P(DP), P(DP), P(DP)),
        out_specs=(P(ALL), P(DP), P(), P(DP)),
        check_vma=False,
    )
```

time: 280 us -> 115 us (0.41)
  Pallas kernels: 0 us -> 109 us
  waiting for transfers between devices: 105 us -> 0 us
  blocking collectives: 104 us -> 0 us
  matrix products: 31.7 us -> 0 us
  between operations: 14.9 us -> 0.64 us
  other arithmetic: 8.98 us -> 0 us
  starting transfers between devices: 8.21 us -> 0 us
    pallas_call x0 -> x1, Pallas kernels: none -> 109 us  [body(): pl.pallas_call(kernel, out_shape=[jax.ShapeDtypeStruct((1, n), F32) for n...]
    all_gather x1 -> x0, waiting for transfers between devices: 92.3 us -> none  [body(): row_block = lax.all_gather(hidden, DP, axis=0, tiled=True)]
    unnamed x1 -> x0, blocking collectives: 64.5 us -> none
    all_gather x4 -> x0, blocking collectives: 39.2 us -> none  [collected_together(): both, at, found = (lax.all_gather(jnp.concatenate(lines), axis), 0, {})]
    dot_general x2 -> x0, matrix products: 31.7 us -> none  [the longest x1 31.6 us: body(): jnp.dot(row_block, output_weight, preferred_element_type=jnp.float32)]
    all_to_all x2 -> x0, waiting for transfers between devices: 12.2 us -> none  [copy_for_each(): lax.all_to_all(jnp.broadcast_to(value[None], (devices, *value.shape)), ax...]
    all_to_all x2 -> x0, starting transfers between devices: 8.17 us -> none  [copy_for_each(): lax.all_to_all(jnp.broadcast_to(value[None], (devices, *value.shape)), ax...]
    reduce_sum x5 -> x0, other arithmetic: 5.61 us -> none  [the longest x1 3.37 us: block_stats(): expsum = jnp.sum(jnp.exp(logits - largest[:, None]), axis=1)]
  transfers between devices with their start and end apart: 3 -> 0, of which waited for: 3 -> 0; matrix products, arithmetic and copies ran while one was open for 1% -> 0% of each run, Pallas kernels for 0% -> 0%
where the time goes in v1:
time: 115 us
  Pallas kernels  109 us (95%)
  local copies, waits for them, and re-layouts  4.57 us (4%)
    pallas_call x1, Pallas kernels, body(): pl.pallas_call(kernel, out_shape=[jax.ShapeDtypeStruct((1, n), F32) for n...  109 us
    unnamed x4, local copies, waits for them, and re-layouts  4.57 us

profile of v1, /device:TPU:1, one launch (start us, length us, event | category | flops | bytes accessed | tf_op | source)
XLA Modules:
  0.0 114.7 jit_solution(6855498605546279051)
XLA Ops:
  0.6 109.5 %shard_map.102 = (f32[1,24]{1,0:T(1,128)}, f32[1,4]{1,0:T(1,128)}, f32[1,64]{1,0:T(1,128)}, f32[1,16]{1,0:T(1,128)}) custom-call(bf16[192,4096]{1,0:T(8,128)(2,1)} %hid.1, bf16[1002,4096]{1,0:T(8,128)(2,1)} %bitcast.10, s32[1,192]{1,0:T(1,128)} %bitcast.11, s32[1,192]{1,0:T(1,128)} %bitcast.12, f32[1,4]{1,0:T(1,128)} %bitcast.13, f32[1,4]{1,0:T(1,128)} %bitcast.14, ...), custom_call_target="tpu_custom_call" | custom-call | tf_op jit(solution)/shard_map/pallas_call | solution.py:486
  110.1 1.1 copy.15
  111.2 1.1 copy.16
  112.4 1.2 %copy.17 = f32[64]{0:T(128)} copy(f32[64]{0:T(128)} %bitcast.17) | data formatting | bytes 512
  113.5 1.1 copy.18

commit v2 on v1

--- a/solution.py
+++ b/solution.py
@@ -21,7 +21,7 @@
 DIRS = ("+y", "-y", "+z", "-z")
 F32 = jnp.float32
 NT = (((1,), (1,)), ((), ()))
-CUT = 512
+SPLIT = 2
 
 
 ORDER = [
@@ -33,6 +33,7 @@
 GROUPS = len(LAST_SLOT)
 ROWS_G = 256
 N_W = 8
+FAR = (2, 2)
 
 
 def group_of(slot):
@@ -42,6 +43,14 @@
 def moved(n, d):
     k = 1 if d[0] == "+" else -1
     return ((n[0] + (k if d[1] == "y" else 0)) % N, (n[1] + (k if d[1] == "z" else 0)) % N)
+
+
+def before(n, d):
+    return moved(n, ("-" if d[0] == "+" else "+") + d[1])
+
+
+def opposite(s):
+    return ((s[0] + 2) % N, (s[1] + 2) % N)
 
 
 def neg(n):
@@ -76,12 +85,12 @@
     out = own
     for d in children(rot, n):
         out = min(out, due(role, rot, moved(n, d), hop, step) - hop)
-    if role == "M" and n != (0, 0):
+    if role == "M" and n not in ((0, 0), FAR):
         out = min(out, own - hop)
     return out
 
 
-def plan(T=1.45, L=2.1, hop=4.5, step=4.0, half=1.32, horizon=1.6, w_ready=15.0, t0=1.2):
+def plan(T=1.45, L=2.1, hop=4.5, step=4.0, chunk=2.6, horizon=1.6, w_ready=15.0, t0=1.2):
     here = {((0, 0), role, rot): 0.0 for role in "CMO" for rot in range(4)}
     todo = {d: [] for d in DIRS + ("+x", "-x")}
     for role in "CM":
@@ -89,9 +98,11 @@
             for n in ORDER:
                 for d in children(rot, n):
                     todo[d].append((due(role, rot, moved(n, d), hop, step), neg(n), role, rot))
-                if role == "M" and n != (0, 0):
+                if role == "M" and n not in ((0, 0), FAR):
                     late = step * (group_of(POS[neg(n)]) + 1)
                     todo[x_dir(rot)].append((late, neg(n), role, rot))
+    for rot, d in enumerate(DIRS):
+        todo[d].append((step * GROUPS, neg(before(FAR, d)), "O", rot))
     end = {d: 0.0 for d in todo}
     chunks = [(g, w) for g in range(GROUPS) for w in range(2)]
     program, t, w_sent = [], t0, 0
@@ -133,11 +144,11 @@
         now = [c for c in chunks if ready_at(*c) <= t]
         if now:
             chunks.remove(now[0])
-            program.append(("half", *now[0], 0))
-            t += half
-            service(t)
-            program.append(("half", *now[0], 1))
-            t += half
+            for q in range(SPLIT):
+                if q:
+                    service(t)
+                program.append(("step", *now[0], q))
+                t += chunk / SPLIT
         else:
             later = [v for v in here.values() if t < v < 1e8]
             later += [e - horizon for e in end.values() if e - horizon > t]
@@ -180,7 +191,7 @@
             parts.append(ops)
             ops = ready_stats
             ready_stats = []
-            if h == 1:
+            if h == SPLIT - 1:
                 both = [k for k in range(GROUPS) if (k, 0) in done and (k, 1) in done]
                 while told < len(both) and both[told] == told:
                     ops.append(("merge", told))
@@ -205,10 +216,22 @@
     return jnp.sum(v, axis=1, keepdims=True)
 
 
+def pick(j, lo, hi, blocks, run):
+    full = [k for k in range(lo, hi) if blocks[k]]
+    if not full:
+        return
+    if hi - lo == 1:
+        run(blocks[lo])
+        return
+    mid = (lo + hi) // 2
+    pl.when(j < mid)(lambda: pick(j, lo, mid, blocks, run))
+    pl.when(j >= mid)(lambda: pick(j, mid, hi, blocks, run))
+
+
 def kernel(
     hid, wt, tgt, lab, psc, ppr, nxt,
-    o_loss, o_score, o_log, o_weight,
-    hbuf, wbuf, meta_out, meta_in, two, trow, cols, sbuf, merged, st_out, st_in, xs_out, xs_in, lo_out, lo_in,
+    out_ref,
+    hbuf, wbuf, acc, meta_out, meta_in, two, trow, cols, sbuf, merged, st_out, st_in, xs_out, xs_in, lo_out, lo_in,
     h_load, w_load, h_send, h_recv, w_send, w_recv, meta_send, meta_recv, st_send, st_recv, xs_send, xs_recv,
     lo_send, lo_recv,
 ):
@@ -216,17 +239,18 @@
     par = lax.rem(mx, 2)
 
     def device(dy=0, dz=0, dx=0, dc=0):
-        return {
-            "y": lax.rem(my + dy, N),
-            "z": lax.rem(mz + dz, N),
-            "x": lax.rem(mx + dx, N),
-            "c": lax.rem(mc + dc, 2),
-        }
+        y, z, x = lax.rem(my + dy, N), lax.rem(mz + dz, N), lax.rem(mx + dx, N)
+        return ((y * N + z) * N + x) * 2 + lax.rem(mc + dc, 2)
+
+    toward = {
+        "+y": device(dy=1), "-y": device(dy=N - 1), "+z": device(dz=1), "-z": device(dz=N - 1),
+        "+x": device(dx=1), "-x": device(dx=N - 1),
+    }
 
     def remote(src, dst, send, recv, to):
         return pltpu.make_async_remote_copy(
             src_ref=src, dst_ref=dst, send_sem=send, recv_sem=recv, device_id=to,
-            device_id_type=pl.DeviceIdType.MESH,
+            device_id_type=pl.DeviceIdType.LOGICAL,
         )
 
     def wait_for(ref, sem):
@@ -249,9 +273,9 @@
     barrier = pltpu.get_barrier_semaphore()
     plane = [(dy, dz, dc) for dy in range(N) for dz in range(N) for dc in range(2) if (dy, dz, dc) != (0, 0, 0)]
     for dy, dz, dc in plane:
-        pl.semaphore_signal(barrier, inc=1, device_id=device(dy, dz, 0, dc), device_id_type=pl.DeviceIdType.MESH)
+        pl.semaphore_signal(barrier, inc=1, device_id=device(dy, dz, 0, dc), device_id_type=pl.DeviceIdType.LOGICAL)
     for dx in range(1, N):
-        pl.semaphore_signal(barrier, inc=1, device_id=device(0, 0, dx), device_id_type=pl.DeviceIdType.MESH)
+        pl.semaphore_signal(barrier, inc=1, device_id=device(0, 0, dx), device_id_type=pl.DeviceIdType.LOGICAL)
 
     lane = lax.broadcasted_iota(jnp.int32, (8, 128), 1)
     two[...] = jnp.zeros_like(two)
@@ -313,6 +337,11 @@
         for i, v in enumerate((counts, score, prob)):
             cols[i] = jnp.broadcast_to(sum_lanes(v), (K, 128))
 
+    def joined(tiles):
+        top = functools.reduce(jnp.maximum, [t[0:1] for t in tiles])
+        total = functools.reduce(jnp.add, [t[1:2] * jnp.exp(t[0:1] - top) for t in tiles])
+        return top, total, functools.reduce(jnp.add, [t[2:3] for t in tiles])
+
     def run(ops):
         for op in ops:
             if op[0] == "wait":
@@ -322,14 +351,9 @@
             elif op[0] == "send":
                 _, d, role, rot, s = op
                 src, _ = piece(POS[s], role, rot)
-                step = 1 if d[0] == "+" else N - 1
-                if d[1] == "x":
-                    dst, (i, r) = piece(POS[s], role, rot)
-                    to = device(dx=step)
-                else:
-                    dst, (i, r) = piece(POS[neg(moved(neg(s), d))], role, rot)
-                    to = device(dy=step) if d[1] == "y" else device(dz=step)
-                remote(src, dst, h_send, h_recv.at[i, r], to).start()
+                slot = POS[s] if d[1] == "x" else POS[neg(moved(neg(s), d))]
+                dst, (i, r) = piece(slot, role, rot)
+                remote(src, dst, h_send, h_recv.at[i, r], toward[d]).start()
             elif op[0] == "w":
                 rows = pl.ds(op[1] * 128, min(128, COLS - op[1] * 128))
                 remote(
@@ -345,11 +369,8 @@
             elif op[0] == "meta":
                 do_meta()
             elif op[0] == "merge":
-                a, b = sbuf[op[1], 0], sbuf[op[1], 1]
-                top = jnp.maximum(a[0:1], b[0:1])
-                merged[op[1], 0:1] = top
-                merged[op[1], 1:2] = a[1:2] * jnp.exp(a[0:1] - top) + b[1:2] * jnp.exp(b[0:1] - top)
-                merged[op[1], 2:3] = a[2:3] + b[2:3]
+                for i, v in enumerate(joined([sbuf[op[1], q] for q in range(2)])):
+                    merged[op[1], i : i + 1] = v
             elif op[0] == "stat":
                 k = op[1]
                 at = 3 * k
@@ -359,13 +380,13 @@
                 msg = (pltpu.roll(tile, 256 - off, 1) if off else tile)[:, :128]
                 if n < 3:
                     msg = jnp.where(lane < 32 * n, msg, pltpu.roll(merged[g + 1], 32 * n, 1)[:, :128])
-                if ORDER[k] == (0, 0):
-                    st_in[k] = msg
+                if opposite(ORDER[k]) == (0, 0):
+                    st_in[0] = msg
                 else:
                     st_out[k] = msg
             elif op[0] == "stat_send":
                 k = op[1]
-                s = ORDER[k]
+                s = opposite(ORDER[k])
                 if s != (0, 0):
                     i = POS[neg(s)]
                     remote(st_out.at[k], st_in.at[i], st_send, st_recv.at[i], device(s[0], s[1])).start()
@@ -374,54 +395,52 @@
     chunks, parts = segments()
     run(parts[0])
 
-    def stats(g, w, lo, hi, target):
-        rhs = jnp.concatenate([hbuf[pl.ds(8 * g, 8), kq].reshape(ROWS_G, 1024) for kq in range(4)], axis=1)
-        logits = lax.dot_general(wbuf[w, lo:hi], rhs, NT, preferred_element_type=F32)
-        top = jnp.max(logits, axis=0, keepdims=True)
-        total = jnp.sum(jnp.exp(logits - top), axis=0, keepdims=True)
-        row = lax.broadcasted_iota(jnp.int32, logits.shape, 0) + lo
-        picked = jnp.sum(jnp.where(row == target, logits, 0.0), axis=0, keepdims=True)
-        return top, total, picked
+    steps = [(g, w, q) for g, w in chunks for q in range(SPLIT)]
 
     def of(j, values):
-        if all(v == k // 2 for k, v in enumerate(values)):
-            return j // 2
-        if all(v == k % 2 for k, v in enumerate(values)):
-            return j % 2
-        out = 0
-        for k, v in enumerate(values):
-            if v:
-                out += jnp.where(j == k, v, 0)
+        out = jnp.int32(values[0])
+        for k in range(1, len(values)):
+            if values[k] != values[k - 1]:
+                out = jnp.where(j >= k, values[k], out)
         return out
 
-    def chunk(j, _):
-        for k in range(1, len(chunks)):
-            if parts[2 * k]:
-                pl.when(j == k)(functools.partial(run, parts[2 * k]))
-        g, w = of(j, [c[0] for c in chunks]), of(j, [c[1] for c in chunks])
-        core = jnp.where(w == 0, mc, 1 - mc)
-        target = trow[g][0:1] - (base + core * COLS)
-        a = stats(g, w, 0, CUT, target)
-        for k in range(len(chunks)):
-            if parts[2 * k + 1]:
-                pl.when(j == k)(functools.partial(run, parts[2 * k + 1]))
-        b = stats(g, w, CUT, COLS, target)
-        top = jnp.maximum(a[0], b[0])
-        sbuf[g, w, 0:1] = top
-        sbuf[g, w, 1:2] = a[1] * jnp.exp(a[0] - top) + b[1] * jnp.exp(b[0] - top)
-        sbuf[g, w, 2:3] = a[2] + b[2]
+    def step(j, _):
+        pick(j, 0, len(steps), [[]] + parts[1:-1], run)
+        g, w = (of(j, [c[i] for c in steps]) for i in range(2))
+        q = lax.rem(j, SPLIT)
+        per = 4 // SPLIT
+        wide = WIDE // SPLIT
+        rhs = jnp.concatenate(
+            [hbuf[pl.ds(8 * g, 8), q * per + i].reshape(ROWS_G, 1024) for i in range(per)], axis=1
+        )
+        lhs = wbuf[w, :, pl.ds(pl.multiple_of(q * wide, wide), wide)]
+        part = lax.dot_general(lhs, rhs, NT, preferred_element_type=F32)
+
+        @pl.when(q == 0)
+        def _():
+            acc[...] = part
+
+        @pl.when((q > 0) & (q < SPLIT - 1))
+        def _():
+            acc[...] += part
+
+        @pl.when(q == SPLIT - 1)
+        def _():
+            logits = acc[...] + part
+            row = lax.broadcasted_iota(jnp.int32, logits.shape, 0)
+            target = trow[g][0:1] - (base + jnp.where(w == 0, mc, 1 - mc) * COLS)
+            top = jnp.max(logits, axis=0, keepdims=True)
+            sbuf[g, w, 0:1] = top
+            sbuf[g, w, 1:2] = jnp.sum(jnp.exp(logits - top), axis=0, keepdims=True)
+            sbuf[g, w, 2:3] = jnp.sum(jnp.where(row == target, logits, 0.0), axis=0, keepdims=True)
+
         return 0
 
-    lax.fori_loop(0, len(chunks), chunk, 0)
+    lax.fori_loop(0, len(steps), step, 0)
     run(parts[-1])
 
     for k in range(1, 16):
         wait_for(st_in.at[k], st_recv.at[k])
-
-    def joined(tiles):
-        top = functools.reduce(jnp.maximum, [t[0:1] for t in tiles])
-        total = functools.reduce(jnp.add, [t[1:2] * jnp.exp(t[0:1] - top) for t in tiles])
-        return top, total, functools.reduce(jnp.add, [t[2:3] for t in tiles])
 
     for i, v in enumerate(joined([st_in[k] for k in range(16)])):
         xs_out[i : i + 1] = v
@@ -443,7 +462,7 @@
     sums = jnp.zeros((K, 128), F32)
     sub = half_sub.astype(F32)
     for k in range(16):
-        tile = meta_in[k]
+        tile = meta_in[POS[opposite(ORDER[k])]]
         for dc in range(2):
             labels = jnp.where(lax.rem(mc + dc, 2) == 0, tile[1:2], tile[2:3])
             sums += jnp.where(labels == sub, lo_in[2 * k + dc], 0.0)
@@ -458,17 +477,18 @@
     def across(mask, v):
         return jnp.sum(jnp.where(mask, v, 0.0), axis=0, keepdims=True)
 
-    o_score[...] = across(half_lane == half_sub - 4 * dp, score)[:, :4]
-    o_log[...] = across(half_lane == half_sub, log_probs)[:, :K]
+    out_ref[1:2] = across(half_lane == half_sub - 4 * dp, score)
+    out_ref[2:3] = across(half_lane == half_sub, log_probs)
     two[2:3, 0:16] = nxt[...]
     chosen = across(two[2:3, :128] == half_sub, probs)
-    o_weight[...] = (1.0 / (K * chosen))[:, :16]
-    loss = jnp.where(mx // 2 == mc, lo_in[0], lo_in[1])
+    out_ref[3:4] = 1.0 / (K * chosen)
+    own = 2 * POS[2, 2]
+    loss = jnp.where(mx // 2 == mc, lo_in[own], lo_in[own + 1])
     loss = jnp.broadcast_to(loss, (8, 128))
     out = loss
     for q in range(1, 4):
         out = jnp.where(2 * lax.rem(mx, 2) + mc == q, pltpu.roll(loss, 128 - 24 * q, 1), out)
-    o_loss[...] = out[0:1, :24]
+    out_ref[0:1] = out[0:1]
 
     wait_for(hbuf.at[pl.ds(0, 45)], h_send)
     for i in range(N_W):
@@ -480,17 +500,23 @@
     wait_for(lo_in.at[pl.ds(0, 31)], lo_send)
 
 
+def finish(rows, *outs):
+    for i, out in enumerate(outs):
+        out[...] = rows[i : i + 1, : out.shape[1]]
+
+
 def body(hidden, output_weight, targets, labels, prev_scores, prev_probs, next_domains):
     dma = pltpu.SemaphoreType.DMA
     vmem = pl.BlockSpec(memory_space=pltpu.VMEM)
-    outs = pl.pallas_call(
+    rows = pl.pallas_call(
         kernel,
-        out_shape=[jax.ShapeDtypeStruct((1, n), F32) for n in (24, 4, K, 16)],
+        out_shape=jax.ShapeDtypeStruct((8, 128), F32),
         in_specs=[pl.BlockSpec(memory_space=pl.ANY)] * 2 + [vmem] * 5,
-        out_specs=[vmem] * 4,
+        out_specs=vmem,
         scratch_shapes=[
             pltpu.VMEM((48, 4, 32, 1024), jnp.bfloat16),
             pltpu.VMEM((2, COLS, WIDE), jnp.bfloat16),
+            pltpu.VMEM((COLS, ROWS_G), F32),
             pltpu.VMEM((8, 128), F32),
             pltpu.VMEM((16, 8, 128), F32),
             pltpu.VMEM((8, 256), jnp.int32),
@@ -531,6 +557,13 @@
         prev_probs.reshape(1, -1),
         next_domains.reshape(1, -1),
     )
+    sizes = (24, 4, K, 16)
+    outs = pl.pallas_call(
+        finish,
+        out_shape=[jax.ShapeDtypeStruct((1, n), F32) for n in sizes],
+        in_specs=[vmem],
+        out_specs=[vmem] * 4,
+    )(rows)
     return tuple(o.reshape(-1) for o in outs)
 
 

time: 115 us -> 86.2 us (0.75)
  Pallas kernels: 109 us -> 85.4 us
  local copies, waits for them, and re-layouts: 4.57 us -> 0 us
    pallas_call x1 -> x2, Pallas kernels: 109 us -> 85.4 us  [the longest x1 84.2 us: body(): pl.pallas_call(kernel, out_shape=jax.ShapeDtypeStruct((8, 128), F32), in_...]
    unnamed x4 -> x0, local copies, waits for them, and re-layouts: 4.57 us -> none
where the time goes in v2:
time: 86.2 us; the launch traced here: 86.1 us
  Pallas kernels  85.4 us (99%)
    pallas_call x1, Pallas kernels, body(): pl.pallas_call(kernel, out_shape=jax.ShapeDtypeStruct((8, 128), F32), in_...  84.2 us

profile of v2, /device:TPU:1, one launch (start us, length us, event | category | flops | bytes accessed | tf_op | source)
XLA Modules:
  0.0 86.1 jit_solution(4294917059360557763)
XLA Ops:
  0.6 84.2 %shard_map.102.rows = f32[8,128]{1,0:T(8,128)} custom-call(bf16[192,4096]{1,0:T(8,128)(2,1)} %hid.1, bf16[1002,4096]{1,0:T(8,128)(2,1)} %bitcast.10, s32[1,192]{1,0:T(1,128)} %bitcast.11, s32[1,192]{1,0:T(1,128)} %bitcast.12, f32[1,4]{1,0:T(1,128)} %bitcast.13, f32[1,4]{1,0:T(1,128)} %bitcast.14, s32[1,16]{1,0:T(1,128)} %bitcast.15), custom_call_target="tpu_custom_call" | custom-call | tf_op jit(solution)/shard_map/pallas_call | solution.py:511
  84.9 1.2 %shard_map.103 = (f32[1,24]{1,0:T(1,128)}, f32[1,4]{1,0:T(1,128)}, f32[1,64]{1,0:T(1,128)}, f32[1,16]{1,0:T(1,128)}) custom-call(f32[8,128]{1,0:T(8,128)} %shard_map.102.rows), custom_call_target="tpu_custom_call" | custom-call | tf_op jit(solution)/shard_map/pallas_call | solution.py:561

commit v3 on v2

--- a/solution.py
+++ b/solution.py
@@ -21,7 +21,6 @@
 DIRS = ("+y", "-y", "+z", "-z")
 F32 = jnp.float32
 NT = (((1,), (1,)), ((), ()))
-SPLIT = 2
 
 
 ORDER = [
@@ -34,6 +33,7 @@
 ROWS_G = 256
 N_W = 8
 FAR = (2, 2)
+EARLY = 13
 
 
 def group_of(slot):
@@ -77,34 +77,41 @@
 
 
 def x_dir(rot):
-    return "+x" if rot < 2 else "-x"
-
-
-def due(role, rot, n, hop, step):
-    own = step * (group_of(POS[neg(n)]) + 1)
-    out = own
+    return "+x" if rot % 2 == 0 else "-x"
+
+
+def columns_of(role, rot):
+    return rot if role == "C" else (rot + 2) % 4
+
+
+def wanted(role, rot, n, step, lead):
+    return step * (group_of(POS[neg(n)]) + 1) - (lead if columns_of(role, rot) < 2 else 0.0)
+
+
+def due(role, rot, n, hop, step, lead):
+    out = wanted(role, rot, n, step, lead)
     for d in children(rot, n):
-        out = min(out, due(role, rot, moved(n, d), hop, step) - hop)
+        out = min(out, due(role, rot, moved(n, d), hop, step, lead) - hop)
     if role == "M" and n not in ((0, 0), FAR):
-        out = min(out, own - hop)
+        out = min(out, wanted("O", rot, n, step, lead) - hop)
     return out
 
 
-def plan(T=1.45, L=2.1, hop=4.5, step=4.0, chunk=2.6, horizon=1.6, w_ready=15.0, t0=1.2):
+def plan(T=1.45, L=2.7, hop=4.5, step=3.0, lead=2.0, chunk=3.6, horizon=2.2, w_ready=15.0, t0=1.2):
     here = {((0, 0), role, rot): 0.0 for role in "CMO" for rot in range(4)}
     todo = {d: [] for d in DIRS + ("+x", "-x")}
     for role in "CM":
         for rot in range(4):
             for n in ORDER:
                 for d in children(rot, n):
-                    todo[d].append((due(role, rot, moved(n, d), hop, step), neg(n), role, rot))
+                    todo[d].append((due(role, rot, moved(n, d), hop, step, lead), neg(n), role, rot))
                 if role == "M" and n not in ((0, 0), FAR):
-                    late = step * (group_of(POS[neg(n)]) + 1)
+                    late = wanted("O", rot, n, step, lead)
                     todo[x_dir(rot)].append((late, neg(n), role, rot))
     for rot, d in enumerate(DIRS):
-        todo[d].append((step * GROUPS, neg(before(FAR, d)), "O", rot))
+        todo[d].append((wanted("O", rot, FAR, step, lead), neg(before(FAR, d)), "O", rot))
     end = {d: 0.0 for d in todo}
-    chunks = [(g, w) for g in range(GROUPS) for w in range(2)]
+    chunks = [(g, w, q) for g in range(GROUPS) for q in range(2) for w in range(2)]
     program, t, w_sent = [], t0, 0
 
     def service(t):
@@ -130,25 +137,26 @@
                     here[neg(moved(neg(s), d)), role, rot] = end[d] + L
                 program.append(("send", d, role, rot, s))
 
-    def ready_at(g, w):
+    def ready_at(g, w, q):
         last = max(
             here.get((s, role, rot), 1e9)
             for s in ORDER[: LAST_SLOT[g] + 1]
             for role in "CMO"
             for rot in range(4)
+            if columns_of(role, rot) // 2 == q
         )
         return max(last, w_ready if w else 3.5)
 
+    def free(g, w, q):
+        return ((g, w, 0) if q else (g - 2, w, 1)) not in chunks
+
     while any(todo.values()) or chunks:
         service(t)
-        now = [c for c in chunks if ready_at(*c) <= t]
+        now = [c for c in chunks if ready_at(*c) <= t and free(*c)]
         if now:
             chunks.remove(now[0])
-            for q in range(SPLIT):
-                if q:
-                    service(t)
-                program.append(("step", *now[0], q))
-                t += chunk / SPLIT
+            program.append(("step", *now[0]))
+            t += chunk / 2
         else:
             later = [v for v in here.values() if t < v < 1e8]
             later += [e - horizon for e in end.values() if e - horizon > t]
@@ -175,24 +183,24 @@
         elif op[0] == "w":
             ops.append(op)
         else:
-            _, g, w, h = op
-            if h == 0:
-                if "meta" not in flags:
-                    flags.add("meta")
-                    ops.append(("meta",))
-                if w not in flags:
-                    flags.add(w)
-                    ops.append(("w_wait", w))
-                for s in ORDER[: LAST_SLOT[g] + 1]:
-                    for role in "CMO":
-                        for rot in range(4):
+            _, g, w, q = op
+            if "meta" not in flags:
+                flags.add("meta")
+                ops.append(("meta",))
+            if w not in flags:
+                flags.add(w)
+                ops.append(("w_wait", w))
+            for s in ORDER[: LAST_SLOT[g] + 1]:
+                for role in "CMO":
+                    for rot in range(4):
+                        if columns_of(role, rot) // 2 == q:
                             need(s, role, rot)
-                done.append((g, w))
+            done.append((g, w, q))
             parts.append(ops)
             ops = ready_stats
             ready_stats = []
-            if h == SPLIT - 1:
-                both = [k for k in range(GROUPS) if (k, 0) in done and (k, 1) in done]
+            if q == 1:
+                both = [k for k in range(GROUPS) if (k, 0, 1) in done and (k, 1, 1) in done]
                 while told < len(both) and both[told] == told:
                     ops.append(("merge", told))
                     lo = 8 * told
@@ -203,6 +211,8 @@
                     told += 1
     parts.append(ops)
     parts[-1] += ready_stats
+    assert any(("stat_send", EARLY - 1) in p for p in parts[:-1])
+    parts[-2] = parts[-2] + [("early",)]
     return done, parts
 
 
@@ -231,8 +241,8 @@
 def kernel(
     hid, wt, tgt, lab, psc, ppr, nxt,
     out_ref,
-    hbuf, wbuf, acc, meta_out, meta_in, two, trow, cols, sbuf, merged, st_out, st_in, xs_out, xs_in, lo_out, lo_in,
-    h_load, w_load, h_send, h_recv, w_send, w_recv, meta_send, meta_recv, st_send, st_recv, xs_send, xs_recv,
+    hbuf, wbuf, acc, meta_out, meta_in, two, trow, cols, sbuf, merged, st_out, st_in, lt_in, xs_out, xs_in, lo_out, lo_in,
+    h_load, w_load, h_send, h_recv, w_send, w_recv, meta_send, meta_recv, st_send, st_recv, lt_send, lt_recv, xs_send, xs_recv,
     lo_send, lo_recv,
 ):
     my, mz, mx, mc = (lax.axis_index(a) for a in ALL)
@@ -274,8 +284,9 @@
     plane = [(dy, dz, dc) for dy in range(N) for dz in range(N) for dc in range(2) if (dy, dz, dc) != (0, 0, 0)]
     for dy, dz, dc in plane:
         pl.semaphore_signal(barrier, inc=1, device_id=device(dy, dz, 0, dc), device_id_type=pl.DeviceIdType.LOGICAL)
-    for dx in range(1, N):
-        pl.semaphore_signal(barrier, inc=1, device_id=device(0, 0, dx), device_id_type=pl.DeviceIdType.LOGICAL)
+    beside = [(dy, dz, dx) for dy, dz in ((0, 0), (0, 1), (0, 3), (1, 0), (3, 0)) for dx in range(1, N)]
+    for dy, dz, dx in beside:
+        pl.semaphore_signal(barrier, inc=1, device_id=device(dy, dz, dx), device_id_type=pl.DeviceIdType.LOGICAL)
 
     lane = lax.broadcasted_iota(jnp.int32, (8, 128), 1)
     two[...] = jnp.zeros_like(two)
@@ -293,15 +304,15 @@
     meta_in[POS[0, 0]] = meta_out[...]
     for load in loads:
         load.wait()
-    pl.semaphore_wait(barrier, len(plane) + N - 1)
+    pl.semaphore_wait(barrier, len(plane) + len(beside))
 
     for s in ORDER[1:]:
         k = POS[neg(s)]
         remote(meta_out, meta_in.at[k], meta_send, meta_recv.at[k], device(s[0], s[1])).start()
 
     def piece(slot, role, rot):
-        rg = {"C": 0, "M": 1 + par, "O": 2 - par}[role]
-        return hbuf.at[slot * 3 + rg, rot], (slot * 3 + rg, rot)
+        i = slot * 3 + {"C": 0, "M": 1 + par, "O": 2 - par}[role], columns_of(role, rot)
+        return hbuf.at[i], i
 
     half_sub = lax.broadcasted_iota(jnp.int32, (K, 128), 0)
     half_lane = lax.broadcasted_iota(jnp.int32, (K, 128), 1)
@@ -380,22 +391,35 @@
                 msg = (pltpu.roll(tile, 256 - off, 1) if off else tile)[:, :128]
                 if n < 3:
                     msg = jnp.where(lane < 32 * n, msg, pltpu.roll(merged[g + 1], 32 * n, 1)[:, :128])
-                if opposite(ORDER[k]) == (0, 0):
-                    st_in[0] = msg
-                else:
-                    st_out[k] = msg
+                st_out[k] = msg
+                if ORDER[k] == FAR:
+                    lt_in[k - EARLY, 0] = msg
             elif op[0] == "stat_send":
                 k = op[1]
                 s = opposite(ORDER[k])
-                if s != (0, 0):
-                    i = POS[neg(s)]
-                    remote(st_out.at[k], st_in.at[i], st_send, st_recv.at[i], device(s[0], s[1])).start()
+                if k < EARLY:
+                    remote(st_out.at[k], st_in.at[k], st_send, st_recv.at[k], device(s[0], s[1])).start()
+                else:
+                    for dx in range(N):
+                        if s != (0, 0) or dx:
+                            i = (k - EARLY, (N - dx) % N)
+                            remote(
+                                st_out.at[k], lt_in.at[i], lt_send, lt_recv.at[i], device(s[0], s[1], dx)
+                            ).start()
+            elif op[0] == "early":
+                for k in range(EARLY):
+                    wait_for(st_in.at[k], st_recv.at[k])
+                for i, v in enumerate(joined([st_in[k] for k in range(EARLY)])):
+                    xs_out[i : i + 1] = v
+                xs_in[0] = xs_out[...]
+                for dx in range(1, N):
+                    remote(xs_out, xs_in.at[N - dx], xs_send, xs_recv.at[N - dx], device(dx=dx)).start()
 
     base = ((my * N + mz) * 8 + mx * 2) * COLS
     chunks, parts = segments()
     run(parts[0])
 
-    steps = [(g, w, q) for g, w in chunks for q in range(SPLIT)]
+    steps = chunks
 
     def of(j, values):
         out = jnp.int32(values[0])
@@ -406,10 +430,9 @@
 
     def step(j, _):
         pick(j, 0, len(steps), [[]] + parts[1:-1], run)
-        g, w = (of(j, [c[i] for c in steps]) for i in range(2))
-        q = lax.rem(j, SPLIT)
-        per = 4 // SPLIT
-        wide = WIDE // SPLIT
+        g, w, q = (of(j, [c[i] for c in steps]) for i in range(3))
+        per = 2
+        wide = WIDE // 2
         rhs = jnp.concatenate(
             [hbuf[pl.ds(8 * g, 8), q * per + i].reshape(ROWS_G, 1024) for i in range(per)], axis=1
         )
@@ -418,15 +441,11 @@
 
         @pl.when(q == 0)
         def _():
-            acc[...] = part
-
-        @pl.when((q > 0) & (q < SPLIT - 1))
+            acc[lax.rem(g, 2), w] = part
+
+        @pl.when(q == 1)
         def _():
-            acc[...] += part
-
-        @pl.when(q == SPLIT - 1)
-        def _():
-            logits = acc[...] + part
+            logits = acc[lax.rem(g, 2), w] + part
             row = lax.broadcasted_iota(jnp.int32, logits.shape, 0)
             target = trow[g][0:1] - (base + jnp.where(w == 0, mc, 1 - mc) * COLS)
             top = jnp.max(logits, axis=0, keepdims=True)
@@ -439,17 +458,13 @@
     lax.fori_loop(0, len(steps), step, 0)
     run(parts[-1])
 
-    for k in range(1, 16):
-        wait_for(st_in.at[k], st_recv.at[k])
-
-    for i, v in enumerate(joined([st_in[k] for k in range(16)])):
-        xs_out[i : i + 1] = v
-    for dx in range(1, N):
-        remote(xs_out, xs_in.at[N - dx], xs_send, xs_recv.at[N - dx], device(dx=dx)).start()
-    xs_in[0] = xs_out[...]
+    late = [(k, dx) for k in range(16 - EARLY) for dx in range(N)]
+    for k, dx in late:
+        if ORDER[EARLY + k] != FAR or dx:
+            wait_for(lt_in.at[k, dx], lt_recv.at[k, dx])
     for dx in range(1, N):
         wait_for(xs_in.at[dx], xs_recv.at[dx])
-    top, total, picked = joined([xs_in[dx] for dx in range(N)])
+    top, total, picked = joined([xs_in[dx] for dx in range(N)] + [lt_in[k, dx] for k, dx in late])
     loss = top + jnp.log(total) - picked
     lo_out[...] = loss
     for dy, dz, dc in plane:
@@ -495,7 +510,8 @@
         rows = pl.ds(i * 128, min(128, COLS - i * 128))
         wait_for(wbuf.at[1, rows], w_send.at[i])
     wait_for(meta_in.at[pl.ds(0, 15)], meta_send)
-    wait_for(st_in.at[pl.ds(0, 15)], st_send)
+    wait_for(st_in.at[pl.ds(0, EARLY)], st_send)
+    wait_for(st_in.at[pl.ds(0, 11)], lt_send)
     wait_for(xs_in.at[pl.ds(0, 3)], xs_send)
     wait_for(lo_in.at[pl.ds(0, 31)], lo_send)
 
@@ -516,7 +532,7 @@
         scratch_shapes=[
             pltpu.VMEM((48, 4, 32, 1024), jnp.bfloat16),
             pltpu.VMEM((2, COLS, WIDE), jnp.bfloat16),
-            pltpu.VMEM((COLS, ROWS_G), F32),
+            pltpu.VMEM((2, 2, COLS, ROWS_G), F32),
             pltpu.VMEM((8, 128), F32),
             pltpu.VMEM((16, 8, 128), F32),
             pltpu.VMEM((8, 256), jnp.int32),
@@ -526,6 +542,7 @@
             pltpu.VMEM((GROUPS, 8, 256), F32),
             pltpu.VMEM((16, 8, 128), F32),
             pltpu.VMEM((16, 8, 128), F32),
+            pltpu.VMEM((16 - EARLY, N, 8, 128), F32),
             pltpu.VMEM((8, 128), F32),
             pltpu.VMEM((N, 8, 128), F32),
             pltpu.VMEM((1, 128), F32),
@@ -540,6 +557,8 @@
             dma((16,)),
             dma(()),
             dma((16,)),
+            dma(()),
+            dma((16 - EARLY, N)),
             dma(()),
             dma((N,)),
             dma(()),

time: 86.2 us -> 80.8 us (0.937)
  Pallas kernels: 85.4 us -> 80 us
    pallas_call x1, Pallas kernels: 84.2 us -> 78.8 us  [body(): pl.pallas_call(kernel, out_shape=jax.ShapeDtypeStruct((8, 128), F32), in_...]
where the time goes in v3:
time: 80.8 us; the launch traced here: 80.7 us
  Pallas kernels  80 us (99%)
    pallas_call x1, Pallas kernels, body(): pl.pallas_call(kernel, out_shape=jax.ShapeDtypeStruct((8, 128), F32), in_...  78.8 us

profile of v3, /device:TPU:1, one launch (start us, length us, event | category | flops | bytes accessed | tf_op | source)
XLA Modules:
  0.0 80.7 jit_solution(10429994960232550741)
XLA Ops:
  0.6 78.8 %shard_map.102.rows = f32[8,128]{1,0:T(8,128)} custom-call(bf16[192,4096]{1,0:T(8,128)(2,1)} %hid.1, bf16[1002,4096]{1,0:T(8,128)(2,1)} %bitcast.10, s32[1,192]{1,0:T(1,128)} %bitcast.11, s32[1,192]{1,0:T(1,128)} %bitcast.12, f32[1,4]{1,0:T(1,128)} %bitcast.13, f32[1,4]{1,0:T(1,128)} %bitcast.14, s32[1,16]{1,0:T(1,128)} %bitcast.15), custom_call_target="tpu_custom_call" | custom-call | tf_op jit(solution)/shard_map/pallas_call | solution.py:527
  79.5 1.2 %shard_map.103 = (f32[1,24]{1,0:T(1,128)}, f32[1,4]{1,0:T(1,128)}, f32[1,64]{1,0:T(1,128)}, f32[1,16]{1,0:T(1,128)}) custom-call(f32[8,128]{1,0:T(8,128)} %shard_map.102.rows), custom_call_target="tpu_custom_call" | custom-call | tf_op jit(solution)/shard_map/pallas_call | solution.py:580

commit v4 on v3

--- a/solution.py
+++ b/solution.py
@@ -51,6 +51,10 @@
 
 def opposite(s):
     return ((s[0] + 2) % N, (s[1] + 2) % N)
+
+
+def hops(*offsets):
+    return sum(min(k, N - k) for k in offsets)
 
 
 def neg(n):
@@ -282,9 +286,11 @@
 
     barrier = pltpu.get_barrier_semaphore()
     plane = [(dy, dz, dc) for dy in range(N) for dz in range(N) for dc in range(2) if (dy, dz, dc) != (0, 0, 0)]
+    plane.sort(key=lambda p: -hops(*p))
     for dy, dz, dc in plane:
         pl.semaphore_signal(barrier, inc=1, device_id=device(dy, dz, 0, dc), device_id_type=pl.DeviceIdType.LOGICAL)
     beside = [(dy, dz, dx) for dy, dz in ((0, 0), (0, 1), (0, 3), (1, 0), (3, 0)) for dx in range(1, N)]
+    beside.sort(key=lambda p: -hops(*p))
     for dy, dz, dx in beside:
         pl.semaphore_signal(barrier, inc=1, device_id=device(dy, dz, dx), device_id_type=pl.DeviceIdType.LOGICAL)
 
@@ -400,7 +406,7 @@
                 if k < EARLY:
                     remote(st_out.at[k], st_in.at[k], st_send, st_recv.at[k], device(s[0], s[1])).start()
                 else:
-                    for dx in range(N):
+                    for dx in (2, 1, 3, 0):
                         if s != (0, 0) or dx:
                             i = (k - EARLY, (N - dx) % N)
                             remote(

time: 80.8 us -> 80.6 us (level)
  no operation moved by 1% of the time
where the time goes in v4:
time: 80.6 us; the launch traced here: 80.4 us
  Pallas kernels  79.8 us (99%)
    pallas_call x1, Pallas kernels, body(): pl.pallas_call(kernel, out_shape=jax.ShapeDtypeStruct((8, 128), F32), in_...  78.6 us

profile of v4, /device:TPU:1, one launch (start us, length us, event | category | flops | bytes accessed | tf_op | source)
XLA Modules:
  0.0 80.4 jit_solution(1058271234435069037)
XLA Ops:
  0.6 78.6 %shard_map.102.rows = f32[8,128]{1,0:T(8,128)} custom-call(bf16[192,4096]{1,0:T(8,128)(2,1)} %hid.1, bf16[1002,4096]{1,0:T(8,128)(2,1)} %bitcast.10, s32[1,192]{1,0:T(1,128)} %bitcast.11, s32[1,192]{1,0:T(1,128)} %bitcast.12, f32[1,4]{1,0:T(1,128)} %bitcast.13, f32[1,4]{1,0:T(1,128)} %bitcast.14, s32[1,16]{1,0:T(1,128)} %bitcast.15), custom_call_target="tpu_custom_call" | custom-call | tf_op jit(solution)/shard_map/pallas_call | solution.py:533
  79.2 1.2 %shard_map.103 = (f32[1,24]{1,0:T(1,128)}, f32[1,4]{1,0:T(1,128)}, f32[1,64]{1,0:T(1,128)}, f32[1,16]{1,0:T(1,128)}) custom-call(f32[8,128]{1,0:T(8,128)} %shard_map.102.rows), custom_call_target="tpu_custom_call" | custom-call | tf_op jit(solution)/shard_map/pallas_call | solution.py:586
